TPU v7x, 32 devices: a whole 2x2x4 slice. The times are simulated.
32 devices in a mesh: band: 8 (over z, x), space: 4 (over y, core).
Axes of the slice: x: 2, y: 2, z: 4, core: 2. Of those that a mesh axis runs over, the one named last changes fastest.
Arguments:
- orbitals: bfloat16 [64, 64, 160, 128], P('band', None, 'space'), may hold values from -8.5 to 8.5
- occupations: float32 [64], P('band'), may hold values from 0.07 to 2.5
Outputs:
- potential: float32 [64, 160, 128], P('band', 'space')
All inputs are finite; a program needn't handle non-finite values.
Results may differ from a plain program's by a relative error of at most 0.0003.
Values sent between devices are 32-bit elements; how exact they have to be, the bound alone decides.
A program may use at most 64 MiB of HBM per device.

v0:
```python
import math
import jax
import jax.numpy as jnp
from jax import lax
from jax.sharding import PartitionSpec as P

ITERS = 3
four_pi = 4.0 * math.pi


def with_halo(shard, sides, width):
    for axis, dim in sides:
        peers, length = (lax.axis_size(axis), shard.shape[dim])
        up = [(i, (i + 1) % peers) for i in range(peers - 1)]
        down = [(j, i) for i, j in up]
        last = lax.slice_in_dim(shard, length - width, length, axis=dim)
        first = lax.slice_in_dim(shard, 0, width, axis=dim)
        before = lax.ppermute(last, axis, up)
        after = lax.ppermute(first, axis, down)
        shard = jnp.concatenate([before, shard, after], axis=dim)
    return shard


def stencil(padded):
    center = padded[2:-2, 2:-2, 2:-2]
    near = padded[3:-1, 2:-2, 2:-2] + padded[1:-3, 2:-2, 2:-2]
    near = near + padded[2:-2, 3:-1, 2:-2] + padded[2:-2, 1:-3, 2:-2]
    near = near + padded[2:-2, 2:-2, 3:-1] + padded[2:-2, 2:-2, 1:-3]
    distant = padded[4:, 2:-2, 2:-2] + padded[:-4, 2:-2, 2:-2]
    distant = distant + padded[2:-2, 4:, 2:-2] + padded[2:-2, :-4, 2:-2]
    distant = distant + padded[2:-2, 2:-2, 4:] + padded[2:-2, 2:-2, :-4]
    return 7.5 * center - 4.0 / 3.0 * near + 1.0 / 12.0 * distant


def operate(field):
    widened = with_halo(field, (("band", 0), ("space", 1)), 2)
    return stencil(jnp.pad(widened, ((0, 0), (0, 0), (2, 2))))


def paired_sums(residual, image):
    return lax.psum((jnp.sum(residual * residual), jnp.sum(residual * image)), ("band", "space"))


def local(orbitals, occupations):

    def accumulate(index, total):
        wave = lax.dynamic_index_in_dim(orbitals, index, 0, keepdims=False).astype(jnp.float32)
        return total + occupations[index] * wave * wave

    start = jnp.zeros(orbitals.shape[1:], jnp.float32)
    partial_value = lax.fori_loop(0, orbitals.shape[0], accumulate, start)
    groups = lax.axis_size("band")
    summed = lax.psum(partial_value, "band")
    share = orbitals.shape[1] // groups
    mine = lax.dynamic_slice_in_dim(summed, lax.axis_index("band") * share, share, 0)
    density = mine / (orbitals.shape[0] * groups)
    source = four_pi * density
    potential = jnp.zeros_like(source)
    residual = source
    image = operate(residual)
    norm_now, product = paired_sums(residual, image)
    alpha = norm_now / product
    direction, along = (residual, image)
    for step in range(ITERS):
        potential = potential + alpha * direction
        residual = residual - alpha * along
        if step + 1 < ITERS:
            image = operate(residual)
            norm_next, product = paired_sums(residual, image)
            ratio = norm_next / norm_now
            alpha = norm_next / (product - ratio * norm_next / alpha)
            direction = residual + ratio * direction
            along = image + ratio * along
            norm_now = norm_next
    return potential


def solution(mesh):
    in_specs = (P("band", None, "space", None), P("band"))
    out_specs = P("band", "space", None)
    return jax.shard_map(local, mesh=mesh, in_specs=in_specs, out_specs=out_specs, check_vma=False)
```

profile of v0, /device:TPU:0, one launch (start us, length us, event | category | flops | bytes accessed | tf_op | source)
XLA Modules:
  0.0 320.6 jit_solution(14691085561565989361)
XLA Ops:
  6.5 30.2 %while.14 = (s32[]{:T(128)}, f32[64,40,128]{2,1,0:T(8,128)S(1)}, f32[8]{0:T(128)}, bf16[8,64,40,128]{3,2,1,0:T(8,128)(2,1)}, s32[]{:T(128)}, /*index=5*/s32[]{:T(128)}) while((s32[]{:T(128)}, f32[64,40,128]{2,1,0:T(8,128)S(1)}, f32[8]{0:T(128)}, bf16[8,64,40,128]{3,2,1,0:T(8,128)(2,1)}, s32[]{:T(128)}, /*index=5*/s32[]{:T(128)}) %tuple.46), condition=%wide.region_1.2_spmd.clone, body=%wide.region_0.1_spmd.clone.sunk | while | flops 1638403 | bytes 3276907 | solution.py:51
  6.5 1.3 dynamic_slice.31
  7.8 2.5 fusion.46
  10.3 1.3 dynamic_slice.31
  11.6 2.5 fusion.46
  14.1 1.3 dynamic_slice.31
  15.4 2.5 fusion.46
  17.9 1.3 dynamic_slice.31
  19.2 2.5 fusion.46
  21.6 1.3 dynamic_slice.31
  22.9 2.5 fusion.46
  25.4 1.3 dynamic_slice.31
  26.7 2.5 fusion.46
  29.2 1.3 dynamic_slice.31
  30.5 2.5 fusion.46
  33.0 1.3 dynamic_slice.31
  34.3 2.5 fusion.46
  37.9 86.5 %all-reduce.8.cloned.1.call-done = f32[64,40,128]{2,1,0:T(8,128)} async-done(((f32[64,40,128]{2,1,0:T(8,128)}), f32[64,40,128]{2,1,0:T(8,128)}) %all-reduce.8.cloned.1.call-update) | async-done | bytes 1310736 | tf_op jit(solution)/shard_map/psum | solution.py:53
  125.3 3.4 %collective-permute-start.1 = (f32[2,40,128]{2,1,0:T(8,128)S(1)}, f32[2,40,128]{2,1,0:T(8,128)S(1)}, u32[]{:S(2)}, u32[]{:S(2)}) collective-permute-start(f32[2,40,128]{2,1,0:T(8,128)S(1)} %get-tuple-element.138), channel_id=1, source_target_pairs={{0,4},{4,8},{8,12},{12,16},{16,20},{20,24},{24,28},{1,5},{5,9},{9,... | collective-permute-start | bytes 122888 | tf_op jit(solution)/shard_map/ppermute | solution.py:18
  130.3 4.2 %collective-permute-done = f32[2,40,128]{2,1,0:T(8,128)S(1)} collective-permute-done((f32[2,40,128]{2,1,0:T(8,128)S(1)}, f32[2,40,128]{2,1,0:T(8,128)S(1)}, u32[]{:S(2)}, u32[]{:S(2)}) %collective-permute-start) | collective-permute-done | bytes 40992 | tf_op jit(solution)/shard_map/ppermute | solution.py:19
  137.2 3.5 %collective-permute-done.2 = f32[12,2,128]{2,1,0:T(2,128)S(1)} collective-permute-done((f32[12,2,128]{2,1,0:T(2,128)S(1)}, f32[12,2,128]{2,1,0:T(2,128)S(1)}, u32[]{:S(2)}, u32[]{:S(2)}) %collective-permute-start.2) | collective-permute-done | bytes 12320 | tf_op jit(solution)/shard_map/ppermute | solution.py:19
  141.0 1.8 multiply_reduce_fusion.3
  142.8 41.2 %all-reduce.5 = (f32[]{:T(128)}, f32[]{:T(128)}) all-reduce(f32[]{:T(128)} %get-tuple-element.105, f32[]{:T(128)} %get-tuple-element.104), channel_id=1, replica_groups=mesh['band'=8,'space'=4] {'band','space'}, use_global_device_ids=true, to_apply=%region_4.5 | all-reduce | flops 2 | bytes 16 | tf_op jit(solution)/shard_map/psum | solution.py:41
  186.3 4.2 %collective-permute-start.5 = (f32[2,40,128]{2,1,0:T(8,128)S(1)}, f32[2,40,128]{2,1,0:T(8,128)S(1)}, u32[]{:S(2)}, u32[]{:S(2)}) collective-permute-start(f32[2,40,128]{2,1,0:T(8,128)S(1)} %get-tuple-element.136), channel_id=1, source_target_pairs={{0,4},{4,8},{8,12},{12,16},{16,20},{20,24},{24,28},{1,5},{5,9},{9,... | collective-permute-start | bytes 122888 | tf_op jit(solution)/shard_map/ppermute | solution.py:18
  192.1 4.2 %collective-permute-done.4 = f32[2,40,128]{2,1,0:T(8,128)S(1)} collective-permute-done((f32[2,40,128]{2,1,0:T(8,128)S(1)}, f32[2,40,128]{2,1,0:T(8,128)S(1)}, u32[]{:S(2)}, u32[]{:S(2)}) %collective-permute-start.4) | collective-permute-done | bytes 40992 | tf_op jit(solution)/shard_map/ppermute | solution.py:19
  199.0 2.8 collective-permute-done.6
  203.0 41.9 %all-reduce.4 = (f32[]{:T(128)}, f32[]{:T(128)}) all-reduce(f32[]{:T(128)} %get-tuple-element.103, f32[]{:T(128)} %get-tuple-element.102), channel_id=1, replica_groups=mesh['band'=8,'space'=4] {'band','space'}, use_global_device_ids=true, to_apply=%region_8.9 | all-reduce | flops 2 | bytes 16 | tf_op jit(solution)/shard_map/psum | solution.py:41
  249.4 4.2 %collective-permute-start.9 = (f32[2,40,128]{2,1,0:T(8,128)S(1)}, f32[2,40,128]{2,1,0:T(8,128)S(1)}, u32[]{:S(2)}, u32[]{:S(2)}) collective-permute-start(f32[2,40,128]{2,1,0:T(8,128)S(1)} %get-tuple-element.134), channel_id=1, source_target_pairs={{0,4},{4,8},{8,12},{12,16},{16,20},{20,24},{24,28},{1,5},{5,9},{9,... | collective-permute-start | bytes 122888 | tf_op jit(solution)/shard_map/ppermute | solution.py:18
  255.2 4.2 %collective-permute-done.8 = f32[2,40,128]{2,1,0:T(8,128)S(1)} collective-permute-done((f32[2,40,128]{2,1,0:T(8,128)S(1)}, f32[2,40,128]{2,1,0:T(8,128)S(1)}, u32[]{:S(2)}, u32[]{:S(2)}) %collective-permute-start.8) | collective-permute-done | bytes 40992 | tf_op jit(solution)/shard_map/ppermute | solution.py:19
  262.1 3.1 collective-permute-done.10
  266.5 41.9 %all-reduce.3 = (f32[]{:T(128)}, f32[]{:T(128)}) all-reduce(f32[]{:T(128)} %get-tuple-element.101, f32[]{:T(128)} %get-tuple-element.100), channel_id=1, replica_groups=mesh['band'=8,'space'=4] {'band','space'}, use_global_device_ids=true, to_apply=%region_12.13 | all-reduce | flops 2 | bytes 16 | tf_op jit(solution)/shard_map/psum | solution.py:41
  312.1 1.6 multiply_add_fusion
  (37 shorter events, 18.5 us)
Async XLA Ops:
  6.5 117.8 %all-reduce.8.cloned.1.call-start = ((), (), s32[]{:S(2)}) async-start(), calls=%async_computation | async-start | bytes 2621440 | tf_op jit(solution)/shard_map/psum | solution.py:53
  36.7 1.1 copy-start
  125.3 5.0 %collective-permute-start.1 = (f32[2,40,128]{2,1,0:T(8,128)S(1)}, f32[2,40,128]{2,1,0:T(8,128)S(1)}, u32[]{:S(2)}, u32[]{:S(2)}) collective-permute-start(f32[2,40,128]{2,1,0:T(8,128)S(1)} %get-tuple-element.138), channel_id=1, source_target_pairs={{0,4},{4,8},{8,12},{12,16},{16,20},{20,24},{24,28},{1,5},{5,9},{9,... | collective-permute-start | bytes 122888 | tf_op jit(solution)/shard_map/ppermute | solution.py:18
  128.7 5.9 %collective-permute-start = (f32[2,40,128]{2,1,0:T(8,128)S(1)}, f32[2,40,128]{2,1,0:T(8,128)S(1)}, u32[]{:S(2)}, u32[]{:S(2)}) collective-permute-start(f32[2,40,128]{2,1,0:T(8,128)S(1)} %get-tuple-element.139), channel_id=1, source_target_pairs={{4,0},{8,4},{12,8},{16,12},{20,16},{24,20},{28,24},{5,1},{9,5},{13... | collective-permute-start | bytes 122888 | tf_op jit(solution)/shard_map/ppermute | solution.py:19
  134.6 2.6 collective-permute-start.3
  135.9 4.8 %collective-permute-start.2 = (f32[12,2,128]{2,1,0:T(2,128)S(1)}, f32[12,2,128]{2,1,0:T(2,128)S(1)}, u32[]{:S(2)}, u32[]{:S(2)}) collective-permute-start(f32[12,2,128]{2,1,0:T(2,128)S(1)} %get-tuple-element.133), channel_id=1, source_target_pairs={{1,0},{2,1},{3,2},{5,4},{6,5},{7,6},{9,8},{10,9},{11,10},{13,12},{... | collective-permute-start | bytes 36872 | tf_op jit(solution)/shard_map/ppermute | solution.py:19
  186.3 5.8 %collective-permute-start.5 = (f32[2,40,128]{2,1,0:T(8,128)S(1)}, f32[2,40,128]{2,1,0:T(8,128)S(1)}, u32[]{:S(2)}, u32[]{:S(2)}) collective-permute-start(f32[2,40,128]{2,1,0:T(8,128)S(1)} %get-tuple-element.136), channel_id=1, source_target_pairs={{0,4},{4,8},{8,12},{12,16},{16,20},{20,24},{24,28},{1,5},{5,9},{9,... | collective-permute-start | bytes 122888 | tf_op jit(solution)/shard_map/ppermute | solution.py:18
  190.5 5.9 %collective-permute-start.4 = (f32[2,40,128]{2,1,0:T(8,128)S(1)}, f32[2,40,128]{2,1,0:T(8,128)S(1)}, u32[]{:S(2)}, u32[]{:S(2)}) collective-permute-start(f32[2,40,128]{2,1,0:T(8,128)S(1)} %get-tuple-element.137), channel_id=1, source_target_pairs={{4,0},{8,4},{12,8},{16,12},{20,16},{24,20},{28,24},{5,1},{9,5},{13... | collective-permute-start | bytes 122888 | tf_op jit(solution)/shard_map/ppermute | solution.py:19
  196.4 2.6 collective-permute-start.7
  197.7 4.1 %collective-permute-start.6 = (f32[12,2,128]{2,1,0:T(2,128)S(1)}, f32[12,2,128]{2,1,0:T(2,128)S(1)}, u32[]{:S(2)}, u32[]{:S(2)}) collective-permute-start(f32[12,2,128]{2,1,0:T(2,128)S(1)} %get-tuple-element.129), channel_id=1, source_target_pairs={{1,0},{2,1},{3,2},{5,4},{6,5},{7,6},{9,8},{10,9},{11,10},{13,12},{... | collective-permute-start | bytes 36872 | tf_op jit(solution)/shard_map/ppermute | solution.py:19
  249.4 5.8 %collective-permute-start.9 = (f32[2,40,128]{2,1,0:T(8,128)S(1)}, f32[2,40,128]{2,1,0:T(8,128)S(1)}, u32[]{:S(2)}, u32[]{:S(2)}) collective-permute-start(f32[2,40,128]{2,1,0:T(8,128)S(1)} %get-tuple-element.134), channel_id=1, source_target_pairs={{0,4},{4,8},{8,12},{12,16},{16,20},{20,24},{24,28},{1,5},{5,9},{9,... | collective-permute-start | bytes 122888 | tf_op jit(solution)/shard_map/ppermute | solution.py:18
  253.6 5.9 %collective-permute-start.8 = (f32[2,40,128]{2,1,0:T(8,128)S(1)}, f32[2,40,128]{2,1,0:T(8,128)S(1)}, u32[]{:S(2)}, u32[]{:S(2)}) collective-permute-start(f32[2,40,128]{2,1,0:T(8,128)S(1)} %get-tuple-element.135), channel_id=1, source_target_pairs={{4,0},{8,4},{12,8},{16,12},{20,16},{24,20},{28,24},{5,1},{9,5},{13... | collective-permute-start | bytes 122888 | tf_op jit(solution)/shard_map/ppermute | solution.py:19
  259.5 2.6 collective-permute-start.11
  260.8 4.4 %collective-permute-start.10 = (f32[12,2,128]{2,1,0:T(2,128)S(1)}, f32[12,2,128]{2,1,0:T(2,128)S(1)}, u32[]{:S(2)}, u32[]{:S(2)}) collective-permute-start(f32[12,2,128]{2,1,0:T(2,128)S(1)} %get-tuple-element.125), channel_id=1, source_target_pairs={{1,0},{2,1},{3,2},{5,4},{6,5},{7,6},{9,8},{10,9},{11,10},{13,12},{... | collective-permute-start | bytes 36872 | tf_op jit(solution)/shard_map/ppermute | solution.py:19
Sparse Core Ops, SparseCore 0:
  38.0 86.3 all-reduce.7
where the time goes:
time: 322 us; the launch traced here: 321 us
  blocking collectives  125 us (39%)
  waiting for transfers between devices  110 us (34%)
  other arithmetic  27.8 us (9%)
  starting transfers between devices  23.4 us (7%)
  between operations  23 us (7%)
  local copies, waits for them, and re-layouts  11.5 us (4%)
    psum x3, blocking collectives, paired_sums(): lax.psum((jnp.sum(residual * residual), jnp.sum(residual * image)), ('ban...  125 us
    psum x1, waiting for transfers between devices, local(): summed = lax.psum(partial_value, 'band')  86.5 us
    ppermute x6, waiting for transfers between devices, with_halo(): after = lax.ppermute(first, axis, down)  22.1 us
    add x8, other arithmetic, accumulate(): return total + occupations[index] * wave * wave  19.6 us
    ppermute x6, starting transfers between devices, with_halo(): before = lax.ppermute(last, axis, up)  15.6 us
    dynamic_slice x8, local copies, waits for them, and re-layouts, accumulate(): return total + occupations[index] * wave * wave  10.4 us
    ppermute x6, starting transfers between devices, with_halo(): after = lax.ppermute(first, axis, down)  7.75 us
  transfers between devices with their start and end apart: 13, of which 10 were waited for; matrix products, arithmetic and copies ran while one was open for 0% of the time, Pallas kernels for 0%

commit v1 on v0

--- a/solution.py
+++ b/solution.py
@@ -38,7 +38,9 @@
 
 
 def paired_sums(residual, image):
-    return lax.psum((jnp.sum(residual * residual), jnp.sum(residual * image)), ("band", "space"))
+    return jax.lax.psum(
+        jax.lax.psum((jnp.sum(residual * residual), jnp.sum(residual * image)), "space"), "band"
+    )
 
 
 def local(orbitals, occupations):

time: 322 us -> 279 us (0.87)
  blocking collectives: 125 us -> 83.8 us
  starting transfers between devices: 23.4 us -> 19.5 us
    psum x3 -> x6, blocking collectives: 125 us -> 83.8 us  [the longest x3 57.6 us: paired_sums(): jax.lax.psum(jax.lax.psum((jnp.sum(residual * residual), jnp.sum(residual...]
    ppermute x6, starting transfers between devices: 15.6 us -> 11.8 us  [with_halo(): before = lax.ppermute(last, axis, up)]
where the time goes in v1:
time: 279 us; the launch traced here: 278 us
  waiting for transfers between devices  111 us (40%)
  blocking collectives  83.8 us (30%)
  other arithmetic  28.2 us (10%)
  between operations  23.5 us (8%)
  starting transfers between devices  19.5 us (7%)
  local copies, waits for them, and re-layouts  11.7 us (4%)
    psum x1, waiting for transfers between devices, local(): summed = lax.psum(partial_value, 'band')  86.5 us
    psum x3, blocking collectives, paired_sums(): jax.lax.psum(jax.lax.psum((jnp.sum(residual * residual), jnp.sum(residual...  57.6 us
    psum x3, blocking collectives, paired_sums(): jax.lax.psum((jnp.sum(residual * residual), jnp.sum(residual * image)), '...  26.2 us
    ppermute x6, waiting for transfers between devices, with_halo(): after = lax.ppermute(first, axis, down)  23.4 us
    add x8, other arithmetic, accumulate(): return total + occupations[index] * wave * wave  20.1 us
    ppermute x6, starting transfers between devices, with_halo(): before = lax.ppermute(last, axis, up)  11.8 us
    dynamic_slice x8, local copies, waits for them, and re-layouts, accumulate(): return total + occupations[index] * wave * wave  10.6 us
    ppermute x6, starting transfers between devices, with_halo(): after = lax.ppermute(first, axis, down)  7.75 us
  transfers between devices with their start and end apart: 13, of which 10 were waited for; matrix products, arithmetic and copies ran while one was open for 0% of the time, Pallas kernels for 0%

profile of v1, /device:TPU:0, one launch (start us, length us, event | category | flops | bytes accessed | tf_op | source)
XLA Modules:
  0.0 277.8 jit_solution(15871623422627156158)
XLA Ops:
  6.5 30.8 %while.14 = (s32[]{:T(128)}, f32[64,40,128]{2,1,0:T(8,128)S(1)}, f32[8]{0:T(128)}, bf16[8,64,40,128]{3,2,1,0:T(8,128)(2,1)}, s32[]{:T(128)}, /*index=5*/s32[]{:T(128)}) while((s32[]{:T(128)}, f32[64,40,128]{2,1,0:T(8,128)S(1)}, f32[8]{0:T(128)}, bf16[8,64,40,128]{3,2,1,0:T(8,128)(2,1)}, s32[]{:T(128)}, /*index=5*/s32[]{:T(128)}) %tuple.46), condition=%wide.region_1.2_spmd.clone, body=%wide.region_0.1_spmd.clone.sunk | while | flops 1638403 | bytes 3276907 | solution.py:53
  7.9 2.5 fusion.46
  10.4 1.3 dynamic_slice.31
  11.7 2.5 fusion.46
  14.2 1.3 dynamic_slice.31
  15.6 2.5 fusion.46
  18.1 1.3 dynamic_slice.31
  19.4 2.5 fusion.46
  21.9 1.3 dynamic_slice.31
  23.3 2.5 fusion.46
  25.8 1.3 dynamic_slice.31
  27.1 2.5 fusion.46
  31.0 2.5 fusion.46
  34.8 2.5 fusion.46
  38.4 86.5 %all-reduce.11.cloned.1.call-done = f32[64,40,128]{2,1,0:T(8,128)} async-done(((f32[64,40,128]{2,1,0:T(8,128)}), f32[64,40,128]{2,1,0:T(8,128)}) %all-reduce.11.cloned.1.call-update) | async-done | bytes 1310736 | tf_op jit(solution)/shard_map/psum | solution.py:55
  125.9 3.4 %collective-permute-start.1 = (f32[2,40,128]{2,1,0:T(8,128)S(1)}, f32[2,40,128]{2,1,0:T(8,128)S(1)}, u32[]{:S(2)}, u32[]{:S(2)}) collective-permute-start(f32[2,40,128]{2,1,0:T(8,128)S(1)} %get-tuple-element.144), channel_id=1, source_target_pairs={{0,4},{4,8},{8,12},{12,16},{16,20},{20,24},{24,28},{1,5},{5,9},{9,... | collective-permute-start | bytes 122888 | tf_op jit(solution)/shard_map/ppermute | solution.py:18
  130.9 4.2 %collective-permute-done = f32[2,40,128]{2,1,0:T(8,128)S(1)} collective-permute-done((f32[2,40,128]{2,1,0:T(8,128)S(1)}, f32[2,40,128]{2,1,0:T(8,128)S(1)}, u32[]{:S(2)}, u32[]{:S(2)}) %collective-permute-start) | collective-permute-done | bytes 40992 | tf_op jit(solution)/shard_map/ppermute | solution.py:19
  137.8 3.5 %collective-permute-done.2 = f32[12,2,128]{2,1,0:T(2,128)S(1)} collective-permute-done((f32[12,2,128]{2,1,0:T(2,128)S(1)}, f32[12,2,128]{2,1,0:T(2,128)S(1)}, u32[]{:S(2)}, u32[]{:S(2)}) %collective-permute-start.2) | collective-permute-done | bytes 12320 | tf_op jit(solution)/shard_map/ppermute | solution.py:19
  141.6 1.8 multiply_reduce_fusion.3
  143.4 8.7 %all-reduce.8 = (f32[]{:T(128)}, f32[]{:T(128)}) all-reduce(f32[]{:T(128)} %get-tuple-element.105, f32[]{:T(128)} %get-tuple-element.104), channel_id=1, replica_groups=mesh['band'=8,'space'=4] {'space'}, use_global_device_ids=true, to_apply=%region_4.5 | all-reduce | flops 2 | bytes 16 | tf_op jit(solution)/shard_map/psum | solution.py:42
  152.1 19.9 %all-reduce.5 = (f32[]{:T(128)}, f32[]{:T(128)}) all-reduce(f32[]{:T(128)} %get-tuple-element.124, f32[]{:T(128)} %get-tuple-element.125), channel_id=1, replica_groups=mesh['band'=8,'space'=4] {'band'}, use_global_device_ids=true, to_apply=%region_5.6 | all-reduce | flops 2 | bytes 16 | tf_op jit(solution)/shard_map/psum | solution.py:41
  174.2 1.8 collective-permute-start.5
  177.7 4.2 %collective-permute-done.4 = f32[2,40,128]{2,1,0:T(8,128)S(1)} collective-permute-done((f32[2,40,128]{2,1,0:T(8,128)S(1)}, f32[2,40,128]{2,1,0:T(8,128)S(1)}, u32[]{:S(2)}, u32[]{:S(2)}) %collective-permute-start.4) | collective-permute-done | bytes 40992 | tf_op jit(solution)/shard_map/ppermute | solution.py:19
  184.6 3.6 %collective-permute-done.6 = f32[12,2,128]{2,1,0:T(2,128)S(1)} collective-permute-done((f32[12,2,128]{2,1,0:T(2,128)S(1)}, f32[12,2,128]{2,1,0:T(2,128)S(1)}, u32[]{:S(2)}, u32[]{:S(2)}) %collective-permute-start.6) | collective-permute-done | bytes 12320 | tf_op jit(solution)/shard_map/ppermute | solution.py:19
  189.4 8.8 %all-reduce.7 = (f32[]{:T(128)}, f32[]{:T(128)}) all-reduce(f32[]{:T(128)} %get-tuple-element.103, f32[]{:T(128)} %get-tuple-element.102), channel_id=1, replica_groups=mesh['band'=8,'space'=4] {'space'}, use_global_device_ids=true, to_apply=%region_10.11 | all-reduce | flops 2 | bytes 16 | tf_op jit(solution)/shard_map/psum | solution.py:42
  198.2 19.0 %all-reduce.4 = (f32[]{:T(128)}, f32[]{:T(128)}) all-reduce(f32[]{:T(128)} %get-tuple-element.122, f32[]{:T(128)} %get-tuple-element.123), channel_id=1, replica_groups=mesh['band'=8,'space'=4] {'band'}, use_global_device_ids=true, to_apply=%region_11.12 | all-reduce | flops 2 | bytes 16 | tf_op jit(solution)/shard_map/psum | solution.py:41
  221.7 2.7 collective-permute-start.9
  226.1 4.2 %collective-permute-done.8 = f32[2,40,128]{2,1,0:T(8,128)S(1)} collective-permute-done((f32[2,40,128]{2,1,0:T(8,128)S(1)}, f32[2,40,128]{2,1,0:T(8,128)S(1)}, u32[]{:S(2)}, u32[]{:S(2)}) %collective-permute-start.8) | collective-permute-done | bytes 40992 | tf_op jit(solution)/shard_map/ppermute | solution.py:19
  233.0 3.6 %collective-permute-done.10 = f32[12,2,128]{2,1,0:T(2,128)S(1)} collective-permute-done((f32[12,2,128]{2,1,0:T(2,128)S(1)}, f32[12,2,128]{2,1,0:T(2,128)S(1)}, u32[]{:S(2)}, u32[]{:S(2)}) %collective-permute-start.10) | collective-permute-done | bytes 12320 | tf_op jit(solution)/shard_map/ppermute | solution.py:19
  237.9 8.7 %all-reduce.6 = (f32[]{:T(128)}, f32[]{:T(128)}) all-reduce(f32[]{:T(128)} %get-tuple-element.101, f32[]{:T(128)} %get-tuple-element.100), channel_id=1, replica_groups=mesh['band'=8,'space'=4] {'space'}, use_global_device_ids=true, to_apply=%region_16.17 | all-reduce | flops 2 | bytes 16 | tf_op jit(solution)/shard_map/psum | solution.py:42
  246.6 18.7 %all-reduce.3 = (f32[]{:T(128)}, f32[]{:T(128)}) all-reduce(f32[]{:T(128)} %get-tuple-element.120, f32[]{:T(128)} %get-tuple-element.121), channel_id=1, replica_groups=mesh['band'=8,'space'=4] {'band'}, use_global_device_ids=true, to_apply=%region_17.18 | all-reduce | flops 2 | bytes 16 | tf_op jit(solution)/shard_map/psum | solution.py:41
  269.3 1.6 multiply_add_fusion
  (40 shorter events, 22.5 us)
Async XLA Ops:
  6.5 118.4 %all-reduce.11.cloned.1.call-start = ((), (), s32[]{:S(2)}) async-start(), calls=%async_computation | async-start | bytes 2621440 | tf_op jit(solution)/shard_map/psum | solution.py:55
  37.3 1.1 copy-start
  125.9 5.0 %collective-permute-start.1 = (f32[2,40,128]{2,1,0:T(8,128)S(1)}, f32[2,40,128]{2,1,0:T(8,128)S(1)}, u32[]{:S(2)}, u32[]{:S(2)}) collective-permute-start(f32[2,40,128]{2,1,0:T(8,128)S(1)} %get-tuple-element.144), channel_id=1, source_target_pairs={{0,4},{4,8},{8,12},{12,16},{16,20},{20,24},{24,28},{1,5},{5,9},{9,... | collective-permute-start | bytes 122888 | tf_op jit(solution)/shard_map/ppermute | solution.py:18
  129.3 5.9 %collective-permute-start = (f32[2,40,128]{2,1,0:T(8,128)S(1)}, f32[2,40,128]{2,1,0:T(8,128)S(1)}, u32[]{:S(2)}, u32[]{:S(2)}) collective-permute-start(f32[2,40,128]{2,1,0:T(8,128)S(1)} %get-tuple-element.145), channel_id=1, source_target_pairs={{4,0},{8,4},{12,8},{16,12},{20,16},{24,20},{28,24},{5,1},{9,5},{13... | collective-permute-start | bytes 122888 | tf_op jit(solution)/shard_map/ppermute | solution.py:19
  135.2 2.6 collective-permute-start.3
  136.5 4.8 %collective-permute-start.2 = (f32[12,2,128]{2,1,0:T(2,128)S(1)}, f32[12,2,128]{2,1,0:T(2,128)S(1)}, u32[]{:S(2)}, u32[]{:S(2)}) collective-permute-start(f32[12,2,128]{2,1,0:T(2,128)S(1)} %get-tuple-element.139), channel_id=1, source_target_pairs={{1,0},{2,1},{3,2},{5,4},{6,5},{7,6},{9,8},{10,9},{11,10},{13,12},{... | collective-permute-start | bytes 36872 | tf_op jit(solution)/shard_map/ppermute | solution.py:19
  174.2 3.5 %collective-permute-start.5 = (f32[2,40,128]{2,1,0:T(8,128)S(1)}, f32[2,40,128]{2,1,0:T(8,128)S(1)}, u32[]{:S(2)}, u32[]{:S(2)}) collective-permute-start(f32[2,40,128]{2,1,0:T(8,128)S(1)} %get-tuple-element.142), channel_id=1, source_target_pairs={{0,4},{4,8},{8,12},{12,16},{16,20},{20,24},{24,28},{1,5},{5,9},{9,... | collective-permute-start | bytes 122888 | tf_op jit(solution)/shard_map/ppermute | solution.py:18
  176.1 5.9 %collective-permute-start.4 = (f32[2,40,128]{2,1,0:T(8,128)S(1)}, f32[2,40,128]{2,1,0:T(8,128)S(1)}, u32[]{:S(2)}, u32[]{:S(2)}) collective-permute-start(f32[2,40,128]{2,1,0:T(8,128)S(1)} %get-tuple-element.143), channel_id=1, source_target_pairs={{4,0},{8,4},{12,8},{16,12},{20,16},{24,20},{28,24},{5,1},{9,5},{13... | collective-permute-start | bytes 122888 | tf_op jit(solution)/shard_map/ppermute | solution.py:19
  182.0 2.6 collective-permute-start.7
  183.3 4.9 %collective-permute-start.6 = (f32[12,2,128]{2,1,0:T(2,128)S(1)}, f32[12,2,128]{2,1,0:T(2,128)S(1)}, u32[]{:S(2)}, u32[]{:S(2)}) collective-permute-start(f32[12,2,128]{2,1,0:T(2,128)S(1)} %get-tuple-element.135), channel_id=1, source_target_pairs={{1,0},{2,1},{3,2},{5,4},{6,5},{7,6},{9,8},{10,9},{11,10},{13,12},{... | collective-permute-start | bytes 36872 | tf_op jit(solution)/shard_map/ppermute | solution.py:19
  221.7 4.4 %collective-permute-start.9 = (f32[2,40,128]{2,1,0:T(8,128)S(1)}, f32[2,40,128]{2,1,0:T(8,128)S(1)}, u32[]{:S(2)}, u32[]{:S(2)}) collective-permute-start(f32[2,40,128]{2,1,0:T(8,128)S(1)} %get-tuple-element.140), channel_id=1, source_target_pairs={{0,4},{4,8},{8,12},{12,16},{16,20},{20,24},{24,28},{1,5},{5,9},{9,... | collective-permute-start | bytes 122888 | tf_op jit(solution)/shard_map/ppermute | solution.py:18
  224.5 5.9 %collective-permute-start.8 = (f32[2,40,128]{2,1,0:T(8,128)S(1)}, f32[2,40,128]{2,1,0:T(8,128)S(1)}, u32[]{:S(2)}, u32[]{:S(2)}) collective-permute-start(f32[2,40,128]{2,1,0:T(8,128)S(1)} %get-tuple-element.141), channel_id=1, source_target_pairs={{4,0},{8,4},{12,8},{16,12},{20,16},{24,20},{28,24},{5,1},{9,5},{13... | collective-permute-start | bytes 122888 | tf_op jit(solution)/shard_map/ppermute | solution.py:19
  230.4 2.6 collective-permute-start.11
  231.7 4.9 %collective-permute-start.10 = (f32[12,2,128]{2,1,0:T(2,128)S(1)}, f32[12,2,128]{2,1,0:T(2,128)S(1)}, u32[]{:S(2)}, u32[]{:S(2)}) collective-permute-start(f32[12,2,128]{2,1,0:T(2,128)S(1)} %get-tuple-element.131), channel_id=1, source_target_pairs={{1,0},{2,1},{3,2},{5,4},{6,5},{7,6},{9,8},{10,9},{11,10},{13,12},{... | collective-permute-start | bytes 36872 | tf_op jit(solution)/shard_map/ppermute | solution.py:19
Sparse Core Ops, SparseCore 0:
  38.6 86.3 all-reduce.10
